TPU v7x, 256 devices: a whole 4x4x8 slice. The times are simulated.
256 devices in a mesh: shot: 8 (over x_hi, y), rcv: 32 (over x_lo, z, core).
Axes of the slice: x: 4 (x_hi: 2, x_lo: 2; x = x_hi * 2 + x_lo), y: 4, z: 8, core: 2. Of those that a mesh axis runs over, the one named last changes fastest.
Arguments:
- modeled: bfloat16 [2, 64, 8, 256, 512], P(None, 'shot', None, 'rcv'), may hold values from -9 to 9
- observed: bfloat16 [2, 8, 64, 256, 512], P(None, 'shot', 'rcv'), may hold values from -60 to 60
- mask: int32 [64, 8, 256], P('shot', None, 'rcv'), may hold values 0 or 1
- shot_order: int32 [64], replicated, may hold values from 0 to 63, as said below
- line_of_slot: int32 [8], replicated, may hold values from 0 to 7, as said below
- coupling: bfloat16 [2, 512, 512], replicated, may hold values from -0.25 to 0.25
- wavelet: float32 [2, 512], replicated, may hold values from -4 to 4
- damping: float32 [512], replicated, may hold values from 32768 to 524288
Outputs:
- new_wavelet: float32 [2, 512], replicated
- residual_out: bfloat16 [2, 64, 8, 256, 512], P(None, 'shot', None, 'rcv')
Inputs may be any that keep to these rules, and one draw needn't show every extreme that they name: Group g holds the shots shot_order[g * 8] to shot_order[(g + 1) * 8 - 1]; each shot number appears once. `line_of_slot`: each line appears in exactly one slot.
All inputs are finite; a program needn't handle non-finite values. No bound on the sum of `mask` on one device may be relied on, other than what follows from the above.
Results may differ from a plain program's by a relative error of at most 0.00045.
Values may be sent and summed in bfloat16 or wider, within the bound.
No kernel may reach another device: no remote copies, remote signals or barrier semaphores. Data moves between devices by JAX's collectives and lax.ppermute only.
A program may use at most 64 MiB of HBM per device.

v0:
```python
import jax
import jax.numpy as jnp
from jax import lax
from jax.sharding import PartitionSpec as P


def sent_to_all(array, axis):
    size = lax.axis_size(axis)
    return lax.all_to_all(
        jnp.broadcast_to(array[None], (size, *array.shape)), axis, 0, 0, tiled=True
    )


def of_everyone(array, axis):
    return sent_to_all(array, axis).sum(axis=0)


def in_one(arrays, axis):
    ends = [0]
    for a in arrays:
        ends.append(ends[-1] + a.size)
    subtotal = of_everyone(jnp.concatenate([a.ravel() for a in arrays]), axis)
    return tuple((subtotal[b:e].reshape(a.shape) for a, b, e in zip(arrays, ends, ends[1:])))


def weigh(trace, coupling):
    real_part = jnp.dot(trace[0], coupling[0], preferred_element_type=jnp.float32) - jnp.dot(
        trace[1], coupling[1], preferred_element_type=jnp.float32
    )
    imag_part = jnp.dot(trace[0], coupling[1], preferred_element_type=jnp.float32) + jnp.dot(
        trace[1], coupling[0], preferred_element_type=jnp.float32
    )
    return jnp.stack([real_part, imag_part])


def per_device(modeled, observed, mask, shot_order, line_of_slot, coupling, wavelet, damping):
    group_size = modeled.shape[1]
    line_count = modeled.shape[2]
    slot_count = lax.axis_size("shot")
    stored = observed[:, 0]
    spread = lax.all_to_all(stored, "rcv", split_axis=2, concat_axis=1, tiled=True)
    grouped = jnp.take(spread, shot_order, axis=1)
    grouped = grouped.reshape(2, slot_count, group_size, grouped.shape[2], grouped.shape[3])
    arrived = lax.all_to_all(grouped, "shot", split_axis=1, concat_axis=1, tiled=True)
    inverse = (
        jnp.zeros((line_count,), jnp.int32)
        .at[line_of_slot]
        .set(jnp.arange(line_count, dtype=jnp.int32))
    )
    by_line = jnp.transpose(jnp.take(arrived, inverse, axis=1), (0, 2, 1, 3, 4))
    wd = weigh(by_line, coupling)
    wg = weigh(modeled, coupling)
    live = mask.astype(jnp.float32)[..., None]
    res_re = live * (wd[0] - (wavelet[0] * wg[0] - wavelet[1] * wg[1]))
    res_im = live * (wd[1] - (wavelet[0] * wg[1] + wavelet[1] * wg[0]))
    num_re = jnp.sum(wg[0] * res_re + wg[1] * res_im, axis=(0, 1, 2))
    num_im = jnp.sum(wg[0] * res_im - wg[1] * res_re, axis=(0, 1, 2))
    den = jnp.sum(live * (wg[0] * wg[0] + wg[1] * wg[1]), axis=(0, 1, 2))
    numerator = jnp.stack([num_re, num_im])
    numerator, den = in_one((numerator, den), "rcv")
    numerator, den = in_one((numerator, den), "shot")
    new_wavelet = wavelet + numerator / (den + damping)[None, :]
    out_re = live * (wd[0] - (new_wavelet[0] * wg[0] - new_wavelet[1] * wg[1]))
    out_im = live * (wd[1] - (new_wavelet[0] * wg[1] + new_wavelet[1] * wg[0]))
    return (new_wavelet, jnp.stack([out_re, out_im]).astype(jnp.bfloat16))


def solution(mesh):
    placed = (
        P(None, "shot", None, "rcv", None),
        P(None, "shot", "rcv", None, None),
        P("shot", None, "rcv"),
        P(),
        P(),
        P(),
        P(),
        P(),
    )
    return jax.shard_map(
        per_device,
        mesh=mesh,
        in_specs=placed,
        out_specs=(P(), P(None, "shot", None, "rcv", None)),
        check_vma=False,
    )
```

profile of v0, /device:TPU:8, one launch (start us, length us, event | category | flops | bytes accessed | tf_op | source)
XLA Modules:
  0.0 104.6 jit_solution(12052726027214672724)
XLA Ops:
  0.6 3.3 %copy.49 = bf16[2,1,2,256,512]{4,2,0,3,1:T(2,128)(2,1)} copy(bf16[2,1,2,256,512]{4,3,2,1,0:T(8,128)(2,1)} %param.9) | data formatting | bytes 2097152 | tf_op args[1]
  3.9 0.0 copy-start.12
  3.9 0.0 copy-start.7
  3.9 9.9 %all-to-all-start = ((bf16[2,2,256,512]{3,1,0,2:T(2,128)(2,1)}), bf16[2,2,256,512]{3,1,0,2:T(2,128)(2,1)S(1)}, u32[]{:S(2)}, u32[]{:S(2)}) async-start(bf16[2,2,256,512]{3,1,0,2:T(2,128)(2,1)} %bitcast.74), calls=%async_computation | async-start | bytes 2097152 | tf_op jit(solution)/shard_map/all_to_all | solution.py:41
  13.8 0.0 copy-done.12
  13.9 0.1 broadcast_in_dim.43
  13.9 0.0 copy-done.7
  13.9 0.0 copy-start.11
  14.0 0.6 copy-done.11
  14.6 0.6 scatter_custom_fusion
  15.2 0.0 copy-start.8
  15.3 0.6 copy-done.8
  15.9 26.4 %all-to-all-done = bf16[2,2,256,512]{3,1,0,2:T(2,128)(2,1)S(1)} async-done(((bf16[2,2,256,512]{3,1,0,2:T(2,128)(2,1)}), bf16[2,2,256,512]{3,1,0,2:T(2,128)(2,1)S(1)}, u32[]{:S(2)}, u32[]{:S(2)}) %all-to-all-start) | async-done | bytes 1048608 | tf_op jit(solution)/shard_map/all_to_all | solution.py:41
  42.3 0.2 copy.48
  42.5 0.1 copy.29
  42.6 0.6 gather_fusion
  43.3 1.1 %copy_select_fusion.1 = bf16[2,8,8,8,512]{4,3,2,0,1:T(8,128)(2,1)} fusion(bf16[2,8,8,8,512]{4,3,0,2,1:T(8,128)(2,1)S(1)} %bitcast.77, pred[8,8]{1,0:T(8,128)(4,1)S(1)} %broadcast_in_dim.43), kind=kLoop, calls=%fused_computation.10 | loop fusion | flops 524288 | bytes 2097216 | tf_op jit(solution)/shard_map/jit(_take)/select_n | solution.py:42
  44.4 0.0 copy-start
  44.4 0.0 copy-start.4
  44.4 7.2 %all-to-all-start.1 = ((bf16[2,8,8,8,512]{4,3,2,0,1:T(8,128)(2,1)}), bf16[2,8,8,8,512]{4,3,2,0,1:T(8,128)(2,1)S(1)}, u32[]{:S(2)}, u32[]{:S(2)}) async-start(bf16[2,8,8,8,512]{4,3,2,0,1:T(8,128)(2,1)} %copy_select_fusion.1), calls=%async_computation.1 | async-start | bytes 2097152 | tf_op jit(solution)/shard_map/all_to_all | solution.py:44
  51.6 0.0 copy-done
  51.7 0.0 copy-done.4
  51.7 1.4 %fusion.5 = f32[8,8,8,512]{3,2,1,0:T(8,128)} fusion(bf16[2,8,8,8,512]{4,3,2,1,0:T(8,128)(2,1)S(1)} %copy-done.4, bf16[2,512,512]{2,1,0:T(8,128)(2,1)S(1)} %copy-done), kind=kOutput, calls=%fused_computation.26 | convolution fusion | flops 268435456 | bytes 2097152 | tf_op jit(solution)/shard_map/dot_general | solution.py:30
  53.1 0.4 fusion.13
  53.5 1.4 %convolution_subtract_fusion.1 = f32[8,8,8,512]{3,2,1,0:T(8,128)} fusion(f32[8,8,8,512]{3,2,1,0:T(8,128)S(1)} %fusion.13, bf16[2,8,8,8,512]{4,3,2,1,0:T(8,128)(2,1)S(1)} %copy-done.4, bf16[2,512,512]{2,1,0:T(8,128)(2,1)S(1)} %copy-done), kind=kOutput, calls=%fused_computation.6 | convolution fusion | flops 268697600 | bytes 3145728 | tf_op jit(solution)/shard_map/dot_general | solution.py:27
  54.9 9.8 %all-to-all-done.1 = bf16[2,8,8,8,512]{4,3,2,0,1:T(8,128)(2,1)S(1)} async-done(((bf16[2,8,8,8,512]{4,3,2,0,1:T(8,128)(2,1)}), bf16[2,8,8,8,512]{4,3,2,0,1:T(8,128)(2,1)S(1)}, u32[]{:S(2)}, u32[]{:S(2)}) %all-to-all-start.1) | async-done | bytes 1048608 | tf_op jit(solution)/shard_map/all_to_all | solution.py:44
  64.7 0.1 copy.31
  64.8 0.6 gather_fusion.1
  65.4 0.2 fusion
  65.6 0.4 fusion.3
  66.0 0.4 fusion.11
  66.5 0.4 convolution_add_fusion
  66.9 0.0 copy-start.1
  66.9 0.0 copy-start.5
  66.9 0.0 copy-start.6
  66.9 0.4 convolution_subtract_fusion
  67.4 0.0 copy-start.2
  67.4 0.7 copy-done.1
  68.1 0.6 copy-done.5
  68.8 0.4 copy-done.6
  69.1 2.1 %add_reduce_fusion = (f32[512]{0:T(512)S(1)}, f32[512]{0:T(512)S(1)}, f32[512]{0:T(512)S(1)}, f32[8,8,8,512]{3,2,1,0:T(8,128)}) fusion(f32[8,8,8,512]{3,2,1,0:T(8,128)S(1)} %convolution_add_fusion, f32[8,8,8,512]{3,2,1,0:T(8,128)S(1)} %copy-done.1, f32[8,8,8,512]{3,2,1,0:T(8,128)S(1)} %convolution_subtract_fusion, f32[512]{0:T(512)S(1)} %bitcast.83, ...), kind=kOutput, calls=%fused_computation.17 | convolution fusion | flops 274725376 | bytes 6334464 | tf_op jit(solution)/shard_map/dot_general | solution.py:30
  71.3 0.0 copy-done.2
  71.3 0.0 copy-start.3
  71.3 0.1 broadcast_in_dim.48
  71.4 16.8 %all_to_all.35 = f32[32,1,1536]{2,1,0:T(1,128)S(1)} all-to-all(f32[32,1,1536]{2,1,0:T(1,128)S(1)} %broadcast_in_dim.48), channel_id=1, replica_groups=mesh['shot'=8,'rcv'=32] {'rcv'}, dimensions={0} | all-to-all | bytes 393216 | tf_op jit(solution)/shard_map/all_to_all | solution.py:9
  88.2 0.1 reduce_sum.48
  88.4 12.1 %all_to_all.36 = f32[8,1,1536]{2,1,0:T(1,128)S(1)} all-to-all(f32[8,1,1536]{2,1,0:T(1,128)S(1)} %broadcast_in_dim.49), channel_id=1, replica_groups=mesh['shot'=8,'rcv'=32] {'shot'}, dimensions={0} | all-to-all | bytes 98304 | tf_op jit(solution)/shard_map/all_to_all | solution.py:9
  100.6 0.0 copy-start.10
  100.6 0.7 copy-done.10
  101.3 0.0 copy-start.9
  101.3 0.6 copy-done.9
  101.9 0.0 copy-done.3
  101.9 1.6 %fusion.1 = (bf16[1,8,8,8,512]{4,3,2,1,0:T(8,128)(2,1)S(1)}, bf16[1,8,8,8,512]{4,3,2,1,0:T(8,128)(2,1)S(1)}) fusion(f32[8,8,8,512]{3,2,1,0:T(8,128)S(1)} %copy-done.3, f32[8,8,8,512]{3,2,1,0:T(8,128)} %get-tuple-element.11, f32[8,8,8,512]{3,2,1,0:T(8,128)S(1)} %copy-done.1, f32[512]{0:T(512)S(1)} %bitcast.81, f32[512]{0:T(512)S(1)} %bitcast.80, ...), kind=kLoop, calls=%fused_computation.20 | loop fusion | flops 3145728 | bytes 5249024 | tf_op jit(solution)/shard_map/stack | solution.py:65
  103.5 1.1 %pad_maximum_fusion = bf16[2,8,8,8,512]{4,3,2,1,0:T(8,128)(2,1)} fusion(bf16[1,8,8,8,512]{4,3,2,1,0:T(8,128)(2,1)S(1)} %get-tuple-element.6, bf16[1,8,8,8,512]{4,3,2,1,0:T(8,128)(2,1)S(1)} %get-tuple-element.5), kind=kLoop, calls=%fused_computation.7 | loop fusion | flops 524288 | bytes 2097152 | tf_op jit(solution)/shard_map/stack | solution.py:65
  (20 shorter events, 0.2 us)
Async XLA Ops:
  3.9 9.9 %copy-start.12 = (s32[64]{0:T(128)S(1)}, s32[64]{0:T(128)}, u32[]{:S(2)}) copy-start(s32[64]{0:T(128)} %param.11) | copy-start | bytes 772
  3.9 10.0 %copy-start.7 = (s32[8,8,8]{2,1,0:T(8,128)S(1)}, s32[8,8,8]{2,1,0:T(8,128)}, u32[]{:S(2)}) copy-start(s32[8,8,8]{2,1,0:T(8,128)} %param.10) | copy-start | bytes 6148
  3.9 38.4 %all-to-all-start = ((bf16[2,2,256,512]{3,1,0,2:T(2,128)(2,1)}), bf16[2,2,256,512]{3,1,0,2:T(2,128)(2,1)S(1)}, u32[]{:S(2)}, u32[]{:S(2)}) async-start(bf16[2,2,256,512]{3,1,0,2:T(2,128)(2,1)} %bitcast.74), calls=%async_computation | async-start | bytes 2097152 | tf_op jit(solution)/shard_map/all_to_all | solution.py:41
  13.9 0.7 copy-start.11
  15.2 0.7 copy-start.8
  44.4 7.2 %copy-start = (bf16[2,512,512]{2,1,0:T(8,128)(2,1)S(1)}, bf16[2,512,512]{2,1,0:T(8,128)(2,1)}, u32[]{:S(2)}) copy-start(bf16[2,512,512]{2,1,0:T(8,128)(2,1)} %param.13) | copy-start | bytes 3145732
  44.4 7.2 %copy-start.4 = (bf16[2,8,8,8,512]{4,3,2,1,0:T(8,128)(2,1)S(1)}, bf16[2,8,8,8,512]{4,3,2,1,0:T(8,128)(2,1)}, u32[]{:S(2)}) copy-start(bf16[2,8,8,8,512]{4,3,2,1,0:T(8,128)(2,1)} %param.8) | copy-start | bytes 3145732
  44.4 20.3 %all-to-all-start.1 = ((bf16[2,8,8,8,512]{4,3,2,0,1:T(8,128)(2,1)}), bf16[2,8,8,8,512]{4,3,2,0,1:T(8,128)(2,1)S(1)}, u32[]{:S(2)}, u32[]{:S(2)}) async-start(bf16[2,8,8,8,512]{4,3,2,0,1:T(8,128)(2,1)} %copy_select_fusion.1), calls=%async_computation.1 | async-start | bytes 2097152 | tf_op jit(solution)/shard_map/all_to_all | solution.py:44
  66.9 1.2 %copy-start.1 = (f32[8,8,8,512]{3,2,1,0:T(8,128)S(1)}, f32[8,8,8,512]{3,2,1,0:T(8,128)}, u32[]{:S(2)}) copy-start(f32[8,8,8,512]{3,2,1,0:T(8,128)} %convolution_subtract_fusion.1) | copy-start | bytes 3145732
  66.9 1.9 %copy-start.5 = (bf16[2,8,8,8,512]{4,3,2,1,0:T(8,128)(2,1)S(1)}, bf16[2,8,8,8,512]{4,3,2,1,0:T(8,128)(2,1)}, u32[]{:S(2)}) copy-start(bf16[2,8,8,8,512]{4,3,2,1,0:T(8,128)(2,1)} %param.8) | copy-start | bytes 3145732
  66.9 2.2 %copy-start.6 = (f32[8,8,8,512]{3,2,1,0:T(8,128)S(1)}, f32[8,8,8,512]{3,2,1,0:T(8,128)}, u32[]{:S(2)}) copy-start(f32[8,8,8,512]{3,2,1,0:T(8,128)} %fusion.5) | copy-start | bytes 3145732
  67.4 3.9 %copy-start.2 = (f32[8,8,8,512]{3,2,1,0:T(8,128)}, f32[8,8,8,512]{3,2,1,0:T(8,128)S(1)}, u32[]{:S(2)}) copy-start(f32[8,8,8,512]{3,2,1,0:T(8,128)S(1)} %convolution_subtract_fusion) | copy-start | bytes 3145732
  71.3 30.6 %copy-start.3 = (f32[8,8,8,512]{3,2,1,0:T(8,128)S(1)}, f32[8,8,8,512]{3,2,1,0:T(8,128)}, u32[]{:S(2)}) copy-start(f32[8,8,8,512]{3,2,1,0:T(8,128)} %copy-done.2) | copy-start | bytes 3145732
  100.6 0.7 copy-start.10
  101.3 0.6 copy-start.9
where the time goes:
time: 105 us
  waiting for transfers between devices  36.1 us (34%)
  blocking collectives  28.9 us (28%)
  starting transfers between devices  17.1 us (16%)
  local copies, waits for them, and re-layouts  10.1 us (10%)
  matrix products  7.15 us (7%)
  other arithmetic  4.23 us (4%)
    all_to_all x2, blocking collectives, sent_to_all(): lax.all_to_all(jnp.broadcast_to(array[None], (size, *array.shape)), axis,...  28.9 us
    all_to_all x1, waiting for transfers between devices, per_device(): lax.all_to_all(stored, 'rcv', split_axis=2, concat_axis=1, tiled=True)  26.4 us
    all_to_all x1, starting transfers between devices, per_device(): lax.all_to_all(stored, 'rcv', split_axis=2, concat_axis=1, tiled=True)  9.91 us
    all_to_all x1, waiting for transfers between devices, per_device(): lax.all_to_all(grouped, 'shot', split_axis=1, concat_axis=1, tiled=True)  9.76 us
    unnamed x28, local copies, waits for them, and re-layouts  7.58 us
    all_to_all x1, starting transfers between devices, per_device(): lax.all_to_all(grouped, 'shot', split_axis=1, concat_axis=1, tiled=True)  7.21 us
    another operation x2, other arithmetic, per_device(): return (new_wavelet, jnp.stack([out_re, out_im]).astype(jnp.bfloat16))  2.7 us
    dot_general x2, matrix products, weigh(): jnp.dot(trace[1], coupling[0], preferred_element_type=jnp.float32)  2.58 us
  transfers between devices with their start and end apart: 2, of which 2 were waited for; matrix products, arithmetic and copies ran while one was open for 4% of the time, Pallas kernels for 0%

commit v1 on v0

--- a/solution.py
+++ b/solution.py
@@ -41,7 +41,10 @@
     spread = lax.all_to_all(stored, "rcv", split_axis=2, concat_axis=1, tiled=True)
     grouped = jnp.take(spread, shot_order, axis=1)
     grouped = grouped.reshape(2, slot_count, group_size, grouped.shape[2], grouped.shape[3])
-    arrived = lax.all_to_all(grouped, "shot", split_axis=1, concat_axis=1, tiled=True)
+    arrived = jnp.concatenate(
+        lax.all_to_all(jnp.stack(jnp.split(grouped, lax.axis_size("shot"), axis=1)), "shot", 0, 0),
+        axis=1,
+    )
     inverse = (
         jnp.zeros((line_count,), jnp.int32)
         .at[line_of_slot]

time: 105 us -> 109 us (1.038)
  local copies, waits for them, and re-layouts: 10.1 us -> 15.4 us
    unnamed x28 -> x35, local copies, waits for them, and re-layouts: 7.58 us -> 12.2 us
where the time goes in v1:
time: 109 us
  waiting for transfers between devices  36.1 us (33%)
  blocking collectives  28.9 us (27%)
  starting transfers between devices  17.1 us (16%)
  local copies, waits for them, and re-layouts  15.4 us (14%)
  matrix products  7.15 us (7%)
  other arithmetic  3.26 us (3%)
    all_to_all x2, blocking collectives, sent_to_all(): lax.all_to_all(jnp.broadcast_to(array[None], (size, *array.shape)), axis,...  28.9 us
    all_to_all x1, waiting for transfers between devices, per_device(): lax.all_to_all(stored, 'rcv', split_axis=2, concat_axis=1, tiled=True)  26.4 us
    unnamed x35, local copies, waits for them, and re-layouts  12.2 us
    all_to_all x1, starting transfers between devices, per_device(): lax.all_to_all(stored, 'rcv', split_axis=2, concat_axis=1, tiled=True)  9.91 us
    all_to_all x1, waiting for transfers between devices, per_device(): lax.all_to_all(jnp.stack(jnp.split(grouped, lax.axis_size('shot'), axis=1...  9.76 us
    all_to_all x1, starting transfers between devices, per_device(): lax.all_to_all(jnp.stack(jnp.split(grouped, lax.axis_size('shot'), axis=1...  7.21 us
    another operation x2, other arithmetic, per_device(): return (new_wavelet, jnp.stack([out_re, out_im]).astype(jnp.bfloat16))  2.7 us
    dot_general x2, matrix products, weigh(): jnp.dot(trace[1], coupling[0], preferred_element_type=jnp.float32)  2.58 us
  transfers between devices with their start and end apart: 2, of which 2 were waited for; matrix products, arithmetic and copies ran while one was open for 4% of the time, Pallas kernels for 0%

profile of v1, /device:TPU:8, one launch (start us, length us, event | category | flops | bytes accessed | tf_op | source)
XLA Modules:
  0.0 108.9 jit_solution(6524741617067389057)
XLA Ops:
  0.6 3.3 %copy.72 = bf16[2,1,2,256,512]{4,2,0,3,1:T(2,128)(2,1)} copy(bf16[2,1,2,256,512]{4,3,2,1,0:T(8,128)(2,1)} %param.9) | data formatting | bytes 2097152 | tf_op args[1]
  3.9 0.0 copy-start.12
  3.9 0.0 copy-start.7
  3.9 9.9 %all-to-all-start = ((bf16[2,2,256,512]{3,1,0,2:T(2,128)(2,1)}), bf16[2,2,256,512]{3,1,0,2:T(2,128)(2,1)S(1)}, u32[]{:S(2)}, u32[]{:S(2)}) async-start(bf16[2,2,256,512]{3,1,0,2:T(2,128)(2,1)} %bitcast.111), calls=%async_computation | async-start | bytes 2097152 | tf_op jit(solution)/shard_map/all_to_all | solution.py:41
  13.8 0.0 copy-done.12
  13.9 0.1 broadcast_in_dim.43
  13.9 0.0 copy-done.7
  13.9 0.0 copy-start.11
  14.0 0.6 copy-done.11
  14.6 0.6 scatter_custom_fusion
  15.2 0.0 copy-start.8
  15.3 0.6 copy-done.8
  15.9 26.4 %all-to-all-done = bf16[2,2,256,512]{3,1,0,2:T(2,128)(2,1)S(1)} async-done(((bf16[2,2,256,512]{3,1,0,2:T(2,128)(2,1)}), bf16[2,2,256,512]{3,1,0,2:T(2,128)(2,1)S(1)}, u32[]{:S(2)}, u32[]{:S(2)}) %all-to-all-start) | async-done | bytes 1048608 | tf_op jit(solution)/shard_map/all_to_all | solution.py:41
  42.3 0.2 copy.71
  42.5 0.1 copy.50
  42.6 0.6 gather_fusion
  43.3 0.2 copy_select_fusion.1
  43.5 0.7 fusion.38
  44.1 0.7 fusion.37
  44.8 0.7 fusion.36
  45.4 0.7 fusion.35
  46.1 0.7 fusion.34
  46.8 0.7 fusion.33
  47.4 0.7 fusion.32
  48.1 0.7 fusion.31
  48.8 0.0 copy-start
  48.8 0.0 copy-start.4
  48.8 7.2 %all-to-all-start.1 = ((bf16[8,2,1,8,8,512]{5,4,3,1,2,0:T(8,128)(2,1)}), bf16[8,2,1,8,8,512]{5,4,3,1,2,0:T(8,128)(2,1)S(1)}, u32[]{:S(2)}, u32[]{:S(2)}) async-start(bf16[8,2,1,8,8,512]{5,4,3,1,2,0:T(8,128)(2,1)} %fusion.31), calls=%async_computation.1 | async-start | bytes 2097152 | tf_op jit(solution)/shard_map/all_to_all | solution.py:45
  56.0 0.0 copy-done
  56.0 0.0 copy-done.4
  56.0 1.4 %fusion.5 = f32[8,8,8,512]{3,2,1,0:T(8,128)} fusion(bf16[2,8,8,8,512]{4,3,2,1,0:T(8,128)(2,1)S(1)} %copy-done.4, bf16[2,512,512]{2,1,0:T(8,128)(2,1)S(1)} %copy-done), kind=kOutput, calls=%fused_computation.27 | convolution fusion | flops 268435456 | bytes 2097152 | tf_op jit(solution)/shard_map/dot_general | solution.py:30
  57.4 0.4 fusion.13
  57.9 1.4 %convolution_subtract_fusion.1 = f32[8,8,8,512]{3,2,1,0:T(8,128)} fusion(f32[8,8,8,512]{3,2,1,0:T(8,128)S(1)} %fusion.13, bf16[2,8,8,8,512]{4,3,2,1,0:T(8,128)(2,1)S(1)} %copy-done.4, bf16[2,512,512]{2,1,0:T(8,128)(2,1)S(1)} %copy-done), kind=kOutput, calls=%fused_computation.6 | convolution fusion | flops 268697600 | bytes 3145728 | tf_op jit(solution)/shard_map/dot_general | solution.py:27
  59.3 9.8 %all-to-all-done.1 = bf16[8,2,1,8,8,512]{5,4,3,1,2,0:T(8,128)(2,1)S(1)} async-done(((bf16[8,2,1,8,8,512]{5,4,3,1,2,0:T(8,128)(2,1)}), bf16[8,2,1,8,8,512]{5,4,3,1,2,0:T(8,128)(2,1)S(1)}, u32[]{:S(2)}, u32[]{:S(2)}) %all-to-all-start.1) | async-done | bytes 1048608 | tf_op jit(solution)/shard_map/all_to_all | solution.py:45
  69.0 0.1 copy.70
  69.1 0.6 gather_fusion.1
  69.8 0.2 fusion
  69.9 0.4 fusion.3
  70.4 0.4 fusion.11
  70.8 0.4 convolution_add_fusion
  71.2 0.0 copy-start.1
  71.3 0.0 copy-start.5
  71.3 0.0 copy-start.6
  71.3 0.4 convolution_subtract_fusion
  71.7 0.0 copy-start.2
  71.7 0.7 copy-done.1
  72.5 0.7 copy-done.5
  73.1 0.3 copy-done.6
  73.5 2.1 %add_reduce_fusion = (f32[512]{0:T(512)S(1)}, f32[512]{0:T(512)S(1)}, f32[512]{0:T(512)S(1)}, f32[8,8,8,512]{3,2,1,0:T(8,128)}) fusion(f32[8,8,8,512]{3,2,1,0:T(8,128)S(1)} %convolution_add_fusion, f32[8,8,8,512]{3,2,1,0:T(8,128)S(1)} %copy-done.1, f32[8,8,8,512]{3,2,1,0:T(8,128)S(1)} %convolution_subtract_fusion, f32[512]{0:T(512)S(1)} %bitcast.121, ...), kind=kOutput, calls=%fused_computation.18 | convolution fusion | flops 274725376 | bytes 6334464 | tf_op jit(solution)/shard_map/dot_general | solution.py:30
  75.6 0.0 copy-done.2
  75.6 0.0 copy-start.3
  75.7 0.1 broadcast_in_dim.48
  75.8 16.8 %all_to_all.35 = f32[32,1,1536]{2,1,0:T(1,128)S(1)} all-to-all(f32[32,1,1536]{2,1,0:T(1,128)S(1)} %broadcast_in_dim.48), channel_id=1, replica_groups=mesh['shot'=8,'rcv'=32] {'rcv'}, dimensions={0} | all-to-all | bytes 393216 | tf_op jit(solution)/shard_map/all_to_all | solution.py:9
  92.6 0.1 reduce_sum.48
  92.8 12.1 %all_to_all.36 = f32[8,1,1536]{2,1,0:T(1,128)S(1)} all-to-all(f32[8,1,1536]{2,1,0:T(1,128)S(1)} %broadcast_in_dim.49), channel_id=1, replica_groups=mesh['shot'=8,'rcv'=32] {'shot'}, dimensions={0} | all-to-all | bytes 98304 | tf_op jit(solution)/shard_map/all_to_all | solution.py:9
  104.9 0.0 copy-start.10
  105.0 0.7 copy-done.10
  105.6 0.0 copy-start.9
  105.7 0.6 copy-done.9
  106.2 0.0 copy-done.3
  106.2 1.6 %fusion.1 = (bf16[1,8,8,8,512]{4,3,2,1,0:T(8,128)(2,1)S(1)}, bf16[1,8,8,8,512]{4,3,2,1,0:T(8,128)(2,1)S(1)}) fusion(f32[8,8,8,512]{3,2,1,0:T(8,128)S(1)} %copy-done.3, f32[8,8,8,512]{3,2,1,0:T(8,128)} %get-tuple-element.11, f32[8,8,8,512]{3,2,1,0:T(8,128)S(1)} %copy-done.1, f32[512]{0:T(512)S(1)} %bitcast.119, f32[512]{0:T(512)S(1)} %bitcast.118, ...), kind=kLoop, calls=%fused_computation.21 | loop fusion | flops 3145728 | bytes 5249024 | tf_op jit(solution)/shard_map/stack | solution.py:68
  107.9 1.1 pad_maximum_fusion
  (20 shorter events, 0.2 us)
Async XLA Ops:
  3.9 9.9 %copy-start.12 = (s32[64]{0:T(128)S(1)}, s32[64]{0:T(128)}, u32[]{:S(2)}) copy-start(s32[64]{0:T(128)} %param.11) | copy-start | bytes 772
  3.9 10.0 %copy-start.7 = (s32[8,8,8]{2,1,0:T(8,128)S(1)}, s32[8,8,8]{2,1,0:T(8,128)}, u32[]{:S(2)}) copy-start(s32[8,8,8]{2,1,0:T(8,128)} %param.10) | copy-start | bytes 6148
  3.9 38.4 %all-to-all-start = ((bf16[2,2,256,512]{3,1,0,2:T(2,128)(2,1)}), bf16[2,2,256,512]{3,1,0,2:T(2,128)(2,1)S(1)}, u32[]{:S(2)}, u32[]{:S(2)}) async-start(bf16[2,2,256,512]{3,1,0,2:T(2,128)(2,1)} %bitcast.111), calls=%async_computation | async-start | bytes 2097152 | tf_op jit(solution)/shard_map/all_to_all | solution.py:41
  13.9 0.7 copy-start.11
  15.2 0.7 copy-start.8
  48.8 7.2 %copy-start = (bf16[2,512,512]{2,1,0:T(8,128)(2,1)S(1)}, bf16[2,512,512]{2,1,0:T(8,128)(2,1)}, u32[]{:S(2)}) copy-start(bf16[2,512,512]{2,1,0:T(8,128)(2,1)} %param.13) | copy-start | bytes 3145732
  48.8 7.2 %copy-start.4 = (bf16[2,8,8,8,512]{4,3,2,1,0:T(8,128)(2,1)S(1)}, bf16[2,8,8,8,512]{4,3,2,1,0:T(8,128)(2,1)}, u32[]{:S(2)}) copy-start(bf16[2,8,8,8,512]{4,3,2,1,0:T(8,128)(2,1)} %param.8) | copy-start | bytes 3145732
  48.8 20.3 %all-to-all-start.1 = ((bf16[8,2,1,8,8,512]{5,4,3,1,2,0:T(8,128)(2,1)}), bf16[8,2,1,8,8,512]{5,4,3,1,2,0:T(8,128)(2,1)S(1)}, u32[]{:S(2)}, u32[]{:S(2)}) async-start(bf16[8,2,1,8,8,512]{5,4,3,1,2,0:T(8,128)(2,1)} %fusion.31), calls=%async_computation.1 | async-start | bytes 2097152 | tf_op jit(solution)/shard_map/all_to_all | solution.py:45
  71.2 1.2 %copy-start.1 = (f32[8,8,8,512]{3,2,1,0:T(8,128)S(1)}, f32[8,8,8,512]{3,2,1,0:T(8,128)}, u32[]{:S(2)}) copy-start(f32[8,8,8,512]{3,2,1,0:T(8,128)} %convolution_subtract_fusion.1) | copy-start | bytes 3145732
  71.3 1.9 %copy-start.5 = (bf16[2,8,8,8,512]{4,3,2,1,0:T(8,128)(2,1)S(1)}, bf16[2,8,8,8,512]{4,3,2,1,0:T(8,128)(2,1)}, u32[]{:S(2)}) copy-start(bf16[2,8,8,8,512]{4,3,2,1,0:T(8,128)(2,1)} %param.8) | copy-start | bytes 3145732
  71.3 2.2 %copy-start.6 = (f32[8,8,8,512]{3,2,1,0:T(8,128)S(1)}, f32[8,8,8,512]{3,2,1,0:T(8,128)}, u32[]{:S(2)}) copy-start(f32[8,8,8,512]{3,2,1,0:T(8,128)} %fusion.5) | copy-start | bytes 3145732
  71.7 3.9 %copy-start.2 = (f32[8,8,8,512]{3,2,1,0:T(8,128)}, f32[8,8,8,512]{3,2,1,0:T(8,128)S(1)}, u32[]{:S(2)}) copy-start(f32[8,8,8,512]{3,2,1,0:T(8,128)S(1)} %convolution_subtract_fusion) | copy-start | bytes 3145732
  75.6 30.6 %copy-start.3 = (f32[8,8,8,512]{3,2,1,0:T(8,128)S(1)}, f32[8,8,8,512]{3,2,1,0:T(8,128)}, u32[]{:S(2)}) copy-start(f32[8,8,8,512]{3,2,1,0:T(8,128)} %copy-done.2) | copy-start | bytes 3145732
  104.9 0.7 copy-start.10
  105.6 0.6 copy-start.9
